TPU v7x, 512 devices: a whole 4x8x8 slice. The times are simulated.
512 devices in a mesh: space: 64 (over y, x, z_hi), tm: 8 (over z_lo, core).
Axes of the slice: x: 4, y: 8, z: 8 (z_hi: 2, z_lo: 4; z = z_hi * 4 + z_lo), core: 2. Of those that a mesh axis runs over, the one named last changes fastest.
Arguments:
- vectors: bfloat16 [8, 64, 2, 12, 8192], P('tm', None, None, None, 'space'), may hold values from -6 to 6
- dilution: int32 [64], replicated, may hold values from 0 to 23
- gamma_ids: int32 [16], replicated, may hold values from 1 to 15
Outputs:
- gram: float32 [8, 1024, 128], P(None, 'space')
- loops: float32 [8, 1024, 2], P(None, 'space')
All inputs are finite; a program needn't handle non-finite values.
Results may differ from a plain program's by a relative error of at most 0.0003.
Values sent between devices are 32-bit elements; how exact they have to be, the bound alone decides.
A program may use at most 64 MiB of HBM per device.

v0:
```python
from functools import partial
import math

import jax
import jax.numpy as jnp
from jax import lax
from jax.sharding import PartitionSpec as P

TDIL = 2


highest = lax.Precision.HIGHEST


def split_up(value, dim, count):
    before, after = (value.shape[:dim], value.shape[dim + 1 :])
    return jnp.moveaxis(value.reshape(*before, count, -1, *after), dim, 0)


def sent_and_summed(value, axis, dim):
    tiles = split_up(value, dim, lax.axis_size(axis))
    arrived = lax.all_to_all(tiles, axis, split_axis=0, concat_axis=0, tiled=True)
    return arrived.sum(axis=0)


def zero_square():
    return [[0, 0, 0, 0] for _ in range(4)]


def pair_product(left, right):
    real_out = zero_square()
    imag_out = zero_square()
    for row in range(4):
        for col in range(4):
            acc_real = 0
            acc_imag = 0
            for mid in range(4):
                acc_real += (
                    left[0][row][mid] * right[0][mid][col] - left[1][row][mid] * right[1][mid][col]
                )
                acc_imag += (
                    left[0][row][mid] * right[1][mid][col] + left[1][row][mid] * right[0][mid][col]
                )
            real_out[row][col] = acc_real
            imag_out[row][col] = acc_imag
    return (real_out, imag_out)


def dirac_tables():
    factors = [
        (zero_square(), [[0, 0, 0, 1], [0, 0, 1, 0], [0, -1, 0, 0], [-1, 0, 0, 0]]),
        ([[0, 0, 0, -1], [0, 0, 1, 0], [0, 1, 0, 0], [-1, 0, 0, 0]], zero_square()),
        (zero_square(), [[0, 0, 1, 0], [0, 0, 0, -1], [-1, 0, 0, 0], [0, 1, 0, 0]]),
        ([[0, 0, 1, 0], [0, 0, 0, 1], [1, 0, 0, 0], [0, 1, 0, 0]], zero_square()),
    ]
    reals = []
    imags = []
    for number in range(16):
        current = ([[1 if a == b else 0 for b in range(4)] for a in range(4)], zero_square())
        for position in range(4):
            if number >> position & 1:
                current = pair_product(current, factors[position])
        reals.append([value for line in current[0] for value in line])
        imags.append([value for line in current[1] for value in line])
    return (reals, imags)


def pick_gammas(gamma_ids):
    table_real, table_imag = dirac_tables()
    choose = (gamma_ids[:, None] == jnp.arange(16, dtype=jnp.int32)[None, :]).astype(jnp.float32)
    gamma_real = jnp.dot(
        choose, jnp.asarray(table_real, dtype=jnp.float32), precision=highest
    ).reshape(-1, 4, 4)
    gamma_imag = jnp.dot(
        choose, jnp.asarray(table_imag, dtype=jnp.float32), precision=highest
    ).reshape(-1, 4, 4)
    return (gamma_real, gamma_imag)


def shards(vectors, dilution, gamma_ids):
    slices, count, halves, comps, sites = vectors.shape
    owners = lax.axis_size("space")
    total_sites = sites * owners
    gram_scale = 1.0 / math.sqrt(48.0 * total_sites)
    loop_scale = 1.0 / math.sqrt(1.0 * total_sites)
    gamma_real, gamma_imag = pick_gammas(gamma_ids)
    spin_pick = ((dilution % 12 // 3)[:, None] == jnp.arange(4, dtype=jnp.int32)[None, :]).astype(
        jnp.float32
    )
    colour_pick = ((dilution % 3)[:, None] == jnp.arange(3, dtype=jnp.int32)[None, :]).astype(
        jnp.float32
    )
    time_class = dilution // 12
    ein = partial(jnp.einsum, precision=highest)
    lowein = partial(jnp.einsum, preferred_element_type=jnp.float32)
    first_slice = lax.axis_index("tm") * slices
    rows_real = ein("gba,ib->gia", gamma_real, spin_pick)
    rows_imag = ein("gba,ib->gia", gamma_imag, spin_pick)

    def one_slice(inputs):
        block, slice_index = inputs
        spinor = block.reshape(count, 2, 4, 3 * sites)
        real_part = spinor[:, 0]
        imag_part = spinor[:, 1]
        pair_real = lowein("iak,jbk->iajb", real_part, real_part) + lowein(
            "iak,jbk->iajb", imag_part, imag_part
        )
        pair_imag = lowein("iak,jbk->iajb", real_part, imag_part) - lowein(
            "iak,jbk->iajb", imag_part, real_part
        )
        gram_real = ein("gab,iajb->gij", gamma_real, pair_real) - ein(
            "gab,iajb->gij", gamma_imag, pair_imag
        )
        gram_imag = ein("gab,iajb->gij", gamma_real, pair_imag) + ein(
            "gab,iajb->gij", gamma_imag, pair_real
        )
        gram = jnp.concatenate([gram_real, gram_imag], axis=2).reshape(-1, 2 * count)
        gram = gram * gram_scale
        site_sums = jnp.sum(block, axis=-1, dtype=jnp.float32).reshape(count, 2, 4, 3)
        picked = ein("ipac,ic->ipa", site_sums, colour_pick)
        loop_real = ein("gia,ia->gi", rows_real, picked[:, 0]) - ein(
            "gia,ia->gi", rows_imag, picked[:, 1]
        )
        loop_imag = ein("gia,ia->gi", rows_real, picked[:, 1]) + ein(
            "gia,ia->gi", rows_imag, picked[:, 0]
        )
        live = (time_class == slice_index % TDIL).astype(jnp.float32)[None, :]
        loops = jnp.stack([loop_real * live, loop_imag * live], axis=-1).reshape(-1, 2) * loop_scale
        return (gram, loops)

    gram_terms, loop_terms = lax.map(
        one_slice, (vectors, first_slice + jnp.arange(slices, dtype=jnp.int32))
    )
    shares = (sent_and_summed(gram_terms, "space", 1), sent_and_summed(loop_terms, "space", 1))
    gram, loops = (
        lax.all_gather(shares[0], "tm", axis=0, tiled=True),
        lax.all_gather(shares[1], "tm", axis=0, tiled=True),
    )
    return (gram, loops)


def solution(mesh):
    placed = (P("tm", None, None, None, "space"), P(), P())
    return jax.shard_map(
        shards,
        mesh=mesh,
        in_specs=placed,
        out_specs=(P(None, "space", None), P(None, "space", None)),
        check_vma=False,
    )
```

profile of v0, /device:TPU:1, one launch (start us, length us, event | category | flops | bytes accessed | tf_op | source)
XLA Modules:
  0.0 86.8 jit_solution(1026629331614046309)
XLA Ops:
  0.6 0.0 copy-start.4
  0.6 0.0 copy-start.1
  0.7 0.7 copy-done.4
  1.3 0.0 copy-done.1
  1.3 0.0 copy-start.3
  1.3 0.2 fusion.27
  1.5 0.5 copy-done.3
  2.0 0.2 fusion.28
  2.2 1.9 %convert_reduce_fusion = f32[64,2,12]{1,2,0:T(8,128)S(1)} fusion(bf16[1,64,2,12,128]{4,2,3,1,0:T(2,128)(2,1)} %param.5), kind=kLoop, calls=%fused_computation.10 | loop fusion | flops 391680 | bytes 399360 | tf_op jit(solution)/shard_map/while/body/eval_jaxpr/reduce_sum | solution.py:119
  4.2 0.2 copy.58
  4.4 0.0 copy-start.2
  4.4 0.2 copy.72
  4.6 0.5 copy-done.2
  5.1 0.1 fusion.24
  5.1 0.4 fusion.22
  5.6 0.1 fusion.37
  5.6 0.0 copy-start
  5.6 0.1 copy.101
  5.7 0.1 copy.102
  5.8 0.2 convolution_bitcast_fusion.4
  6.0 0.2 multiply_reduce_fusion.3
  6.3 0.1 stack.13
  6.3 0.1 copy.62
  6.4 0.1 stack.12
  6.5 0.1 copy.61
  6.6 0.7 copy.63
  7.3 19.6 %all-to-all-start.1 = ((f32[64,1,16,2]{2,3,1,0:T(2,128)}), f32[64,1,16,2]{2,3,1,0:T(2,128)S(1)}, u32[]{:S(2)}, u32[]{:S(2)}) async-start(f32[64,1,16,2]{2,3,1,0:T(2,128)} %copy.63), calls=%async_computation.1 | async-start | bytes 131072 | tf_op jit(solution)/shard_map/all_to_all | solution.py:22
  26.9 0.0 copy-done
  26.9 0.1 copy.48
  27.0 0.3 reshape.82
  27.2 0.1 fusion.36
  27.4 0.3 fusion.10
  27.7 0.3 fusion.8
  28.0 0.3 convolution_add_fusion
  28.4 0.3 convolution_subtract_fusion
  28.7 1.1 %convolution_bitcast_fusion = f32[16,64,64]{2,0,1:T(8,128)S(1)} fusion(f32[16,4,4,1]{0,2,1,3:T(4,128)S(1)} %bitcast.96, f32[64,4,64,4]{2,0,3,1:T(8,128)S(1)} %convolution_add_fusion), kind=kOutput, calls=%fused_computation | convolution fusion | flops 12582912 | bytes 525312 | tf_op jit(solution)/shard_map/while/body/eval_jaxpr/gab,iajb->gij/dot_general | solution.py:114
  29.8 1.1 %convolution_bitcast_fusion.2 = f32[16,64,64]{2,0,1:T(8,128)S(1)} fusion(f32[16,4,4,1]{0,2,1,3:T(4,128)S(1)} %bitcast.97, f32[64,4,64,4]{2,0,3,1:T(8,128)S(1)} %convolution_subtract_fusion), kind=kOutput, calls=%fused_computation.2 | convolution fusion | flops 12582912 | bytes 525312 | tf_op jit(solution)/shard_map/while/body/eval_jaxpr/gab,iajb->gij/dot_general | solution.py:111
  30.9 1.1 %fusion.1 = f32[16,64,64]{2,0,1:T(8,128)S(1)} fusion(f32[16,64,64]{2,0,1:T(8,128)S(1)} %convolution_bitcast_fusion, f32[16,4,4,1]{0,2,1,3:T(4,128)S(1)} %bitcast.93, f32[64,4,64,4]{2,0,3,1:T(8,128)S(1)} %convolution_subtract_fusion), kind=kOutput, calls=%fused_computation.7 | convolution fusion | flops 12648448 | bytes 787456 | tf_op jit(solution)/shard_map/while/body/eval_jaxpr/gab,iajb->gij/dot_general | solution.py:114
  32.0 1.1 %fusion = f32[16,64,64]{2,0,1:T(8,128)S(1)} fusion(f32[16,64,64]{2,0,1:T(8,128)S(1)} %convolution_bitcast_fusion.2, f32[16,4,4,1]{0,2,1,3:T(4,128)S(1)} %bitcast.94, f32[64,4,64,4]{2,0,3,1:T(8,128)S(1)} %convolution_add_fusion), kind=kOutput, calls=%fused_computation.6 | convolution fusion | flops 12648448 | bytes 787456 | tf_op jit(solution)/shard_map/while/body/eval_jaxpr/gab,iajb->gij/dot_general | solution.py:111
  33.1 0.2 maximum_multiply_fusion
  33.3 1.0 %copy.56 = f32[16,64,128]{2,1,0:T(8,128)} copy(f32[16,64,128]{2,0,1:T(8,128)S(1)} %maximum_multiply_fusion) | data formatting | bytes 1048576 | tf_op jit(solution)/shard_map/while/body/eval_jaxpr/mul | solution.py:118
  34.3 6.1 %all-to-all-done.1 = f32[64,1,16,2]{2,3,1,0:T(2,128)S(1)} async-done(((f32[64,1,16,2]{2,3,1,0:T(2,128)}), f32[64,1,16,2]{2,3,1,0:T(2,128)S(1)}, u32[]{:S(2)}, u32[]{:S(2)}) %all-to-all-start.1) | async-done | bytes 8224 | tf_op jit(solution)/shard_map/all_to_all | solution.py:22
  40.3 8.5 %all-to-all-start = ((f32[64,1,16,128]{3,2,1,0:T(8,128)}), f32[64,1,16,128]{3,2,1,0:T(8,128)S(1)}, u32[]{:S(2)}, u32[]{:S(2)}) async-start(f32[64,1,16,128]{3,2,1,0:T(8,128)} %bitcast.27), calls=%async_computation | async-start | bytes 1048576 | tf_op jit(solution)/shard_map/all_to_all | solution.py:22
  48.8 0.1 reduce_sum.35
  48.9 13.2 %all-gather.2 = f32[8,16,2]{1,2,0:T(2,128)S(1)} all-gather(f32[1,16,2]{1,2,0:T(2,128)S(1)} %bitcast.98), channel_id=3, replica_groups=mesh['space'=64,'tm'=8] {'tm'}, dimensions={0}, use_global_device_ids=true | all-gather | bytes 1152 | tf_op jit(solution)/shard_map/all_gather | solution.py:137
  62.1 5.8 %all-to-all-done = f32[64,1,16,128]{3,2,1,0:T(8,128)S(1)} async-done(((f32[64,1,16,128]{3,2,1,0:T(8,128)}), f32[64,1,16,128]{3,2,1,0:T(8,128)S(1)}, u32[]{:S(2)}, u32[]{:S(2)}) %all-to-all-start) | async-done | bytes 524320 | tf_op jit(solution)/shard_map/all_to_all | solution.py:22
  67.8 0.1 reduce_sum.32
  67.9 17.7 %all-gather = f32[128,128]{1,0:T(8,128)S(1)} all-gather(f32[16,128]{1,0:T(8,128)S(1)} %reduce_sum.32), channel_id=2, replica_groups=mesh['space'=64,'tm'=8] {'tm'}, dimensions={0}, use_global_device_ids=true | all-gather | bytes 73728 | tf_op jit(solution)/shard_map/all_gather | solution.py:136
  85.6 0.6 copy.152
  86.2 0.6 copy.153
  (4 shorter events, 0.1 us)
Async XLA Ops:
  0.6 0.7 copy-start.4
  0.6 0.7 copy-start.1
  1.3 0.7 copy-start.3
  4.4 0.7 copy-start.2
  5.6 21.2 %copy-start = (bf16[1,64,2,12,128]{4,2,3,1,0:T(2,128)(2,1)S(1)}, bf16[1,64,2,12,128]{4,2,3,1,0:T(2,128)(2,1)}, u32[]{:S(2)}) copy-start(bf16[1,64,2,12,128]{4,2,3,1,0:T(2,128)(2,1)} %param.5) | copy-start | bytes 1179652
  7.3 33.0 %all-to-all-start.1 = ((f32[64,1,16,2]{2,3,1,0:T(2,128)}), f32[64,1,16,2]{2,3,1,0:T(2,128)S(1)}, u32[]{:S(2)}, u32[]{:S(2)}) async-start(f32[64,1,16,2]{2,3,1,0:T(2,128)} %copy.63), calls=%async_computation.1 | async-start | bytes 131072 | tf_op jit(solution)/shard_map/all_to_all | solution.py:22
  40.3 27.5 %all-to-all-start = ((f32[64,1,16,128]{3,2,1,0:T(8,128)}), f32[64,1,16,128]{3,2,1,0:T(8,128)S(1)}, u32[]{:S(2)}, u32[]{:S(2)}) async-start(f32[64,1,16,128]{3,2,1,0:T(8,128)} %bitcast.27), calls=%async_computation | async-start | bytes 1048576 | tf_op jit(solution)/shard_map/all_to_all | solution.py:22
where the time goes:
time: 87.2 us; the launch traced here: 86.8 us
  blocking collectives  30.9 us (35%)
  starting transfers between devices  28 us (32%)
  waiting for transfers between devices  11.8 us (14%)
  matrix products  6.86 us (8%)
  local copies, waits for them, and re-layouts  5.96 us (7%)
  other arithmetic  2.42 us (3%)
    all_to_all x2, starting transfers between devices, sent_and_summed(): lax.all_to_all(tiles, axis, split_axis=0, concat_axis=0, tiled=True)  28 us
    all_gather x1, blocking collectives, shards(): lax.all_gather(shares[0], 'tm', axis=0, tiled=True)  17.7 us
    all_gather x1, blocking collectives, shards(): lax.all_gather(shares[1], 'tm', axis=0, tiled=True)  13.2 us
    all_to_all x2, waiting for transfers between devices, sent_and_summed(): lax.all_to_all(tiles, axis, split_axis=0, concat_axis=0, tiled=True)  11.8 us
    unnamed x15, local copies, waits for them, and re-layouts  3.11 us
    reduce_sum x1, other arithmetic, one_slice(): jnp.sum(block, axis=-1, dtype=jnp.float32).reshape(count, 2, 4, 3)  1.93 us
  transfers between devices with their start and end apart: 2, of which 2 were waited for; matrix products, arithmetic and copies ran while one was open for 9% of the time, Pallas kernels for 0%

commit v1 on v0

v1 whole, which is shorter than its diff:
```python
from functools import partial
import math

import jax
import jax.numpy as jnp
import numpy as np
from jax import lax
from jax.experimental import pallas as pl
from jax.experimental.pallas import tpu as pltpu
from jax.sharding import PartitionSpec as P

NV = 64
NG = 16
NY = 8
NX = 4
NZH = 2
NTM = 8
ORDER = (4, 3, 5, 2, 6, 1, 7, 0)
MESH = pl.DeviceIdType.MESH


def dirac_table():
    i = 1j
    gammas = [
        np.array([[0, 0, 0, i], [0, 0, i, 0], [0, -i, 0, 0], [-i, 0, 0, 0]]),
        np.array([[0, 0, 0, -1], [0, 0, 1, 0], [0, 1, 0, 0], [-1, 0, 0, 0]], complex),
        np.array([[0, 0, i, 0], [0, 0, 0, -i], [-i, 0, 0, 0], [0, i, 0, 0]]),
        np.array([[0, 0, 1, 0], [0, 0, 0, 1], [1, 0, 0, 0], [0, 1, 0, 0]], complex),
    ]
    rows = []
    for number in range(16):
        product = np.eye(4, dtype=complex)
        for bit in range(4):
            if number >> bit & 1:
                product = product @ gammas[bit]
        m = int(np.flatnonzero(product[0])[0])
        phase = product[0, m]
        found = None
        for w in range(4):
            signs = [(-1) ** bin(w & a).count("1") for a in range(4)]
            trial = np.zeros((4, 4), complex)
            for a in range(4):
                trial[a, a ^ m] = phase * signs[a]
            if np.array_equal(trial, product):
                found = w
        eps = (-1) ** bin(found & m).count("1")
        rows.append((m, found, int(phase.real), int(phase.imag), eps))
    return rows


TABLE = dirac_table()


def pick(number, values):
    out = jnp.float32(values[0])
    for k in range(1, 16):
        if values[k] != values[0]:
            out = jnp.where(number == k, jnp.float32(values[k]), out)
    return out


def kernel(
    gram_scale,
    loop_scale,
    gid_ref,
    dil_ref,
    v_hbm,
    gram_ref,
    loop_ref,
    vb,
    vf,
    lhs,
    dmat,
    tabs,
    ltab,
    xbuf,
    xrecv,
    ysend,
    yrecv,
    yrecv2,
    zsend,
    zrecv,
    xl,
    xlrecv,
    yl,
    ylrecv,
    zl,
    zlrecv,
    in_sem,
    x_send,
    x_recv,
    y_send,
    y_recv,
    y2_send,
    y2_recv,
    z_send,
    z_recv,
    xl_send,
    xl_recv,
    yl_send,
    yl_recv,
    zl_send,
    zl_recv,
):
    space = lax.axis_index("space")
    tm = lax.axis_index("tm")
    y = space // 8
    x = (space // 2) % 4
    zh = space % 2
    p = x % 2
    xp = x + 1 - 2 * p

    load = pltpu.make_async_copy(v_hbm, vb, in_sem)
    load.start()

    def at(y_, x_, zh_, tm_):
        return (y_ * 8 + x_ * 2 + zh_, tm_)

    barrier = pltpu.get_barrier_semaphore()
    partners = []
    for k in range(1, NX):
        partners.append(at(y, (x + k) % NX, zh, tm))
    for k in range(1, NY):
        partners.append(at((y + k) % NY, x, zh, tm))
        partners.append(at((y + k) % NY, xp, zh, tm))
    for kz in range(NZH):
        for kt in range(NTM):
            if kz or kt:
                partners.append(at(y, x, (zh + kz) % NZH, (tm + kt) % NTM))
    for who in partners:
        pl.semaphore_signal(barrier, inc=1, device_id=who, device_id_type=MESH)

    lane = lax.broadcasted_iota(jnp.int32, (8, 128), 1)
    group = lane // 32
    low = lane < 64
    low1 = lax.broadcasted_iota(jnp.int32, (1, 128), 1) < 64

    load.wait()
    vf[...] = vb[...].astype(jnp.float32)
    for a in range(4):
        for c in range(3):
            start = 2 * (3 * a + c)
            re = vf[pl.ds(start, NV, stride=24), :].astype(jnp.bfloat16)
            im = vf[pl.ds(start + 1, NV, stride=24), :].astype(jnp.bfloat16)
            first = slice(a * 64, a * 64 + 64)
            second = slice(256 + a * 64, 256 + a * 64 + 64)
            kr = slice(c * 128, c * 128 + 128)
            ki = slice((3 + c) * 128, (3 + c) * 128 + 128)
            lhs[first, kr] = re
            lhs[first, ki] = im
            lhs[second, kr] = -im
            lhs[second, ki] = re
    block = lax.broadcasted_iota(jnp.int32, (16, 768), 1) // 128
    row = lax.broadcasted_iota(jnp.int32, (16, 768), 0)
    lhs[512:528, :] = jnp.where(block == row, 1.0, 0.0).astype(jnp.bfloat16)
    prod = lax.dot_general(
        lhs[...], lhs[0:256, :], (((1,), (1,)), ((), ())), preferred_element_type=jnp.float32
    )
    dmat[...] = prod[0:256] + prod[256:512]
    sums = prod[512:528]

    for m in range(4):
        for pp in range(2):
            for qq in range(2):
                parts = []
                for a in range(4):
                    b = a ^ m
                    grp = 2 * (b & 1) + qq
                    tile = None
                    for ib in range(4):
                        r0 = a * 64 + (4 * pp + ib) * 8
                        c0 = (b // 2) * 128
                        piece = dmat[r0 : r0 + 8, c0 : c0 + 128]
                        shift = (32 * (ib - grp)) % 128
                        if shift:
                            piece = pltpu.roll(piece, shift, 1)
                        tile = piece if tile is None else jnp.where(group == ib, piece, tile)
                    parts.append(tile)
                s01, d01 = parts[0] + parts[1], parts[0] - parts[1]
                s23, d23 = parts[2] + parts[3], parts[2] - parts[3]
                combos = (s01 + s23, d01 + d23, s01 - s23, d01 - d23)
                slot = 0 if pp == qq else 1
                for number in range(16):
                    if TABLE[number][0] == m:
                        tabs[number, pp, 8 * slot : 8 * slot + 8, :] = combos[TABLE[number][1]]

    dil = dil_ref[...]
    dil = jnp.concatenate([dil, dil], axis=1)
    klass = (dil >= 12).astype(jnp.int32)
    d12 = dil - 12 * klass
    spin = (
        (d12 >= 3).astype(jnp.int32) + (d12 >= 6).astype(jnp.int32) + (d12 >= 9).astype(jnp.int32)
    )
    colour = d12 - 3 * spin
    live = jnp.where(klass == tm % 2, jnp.float32(loop_scale), jnp.float32(0.0))

    def coloured(h, half):
        out = jnp.zeros((1, 128), jnp.float32)
        for c in range(3):
            line = sums[3 * h + c : 3 * h + c + 1, half * 128 : half * 128 + 128]
            out = out + jnp.where(colour == c, line, 0.0)
        return out

    lines = []
    for half in range(2):
        re, im = coloured(0, half), coloured(1, half)
        lines.append(jnp.where(low1, re, pltpu.roll(im, 64, 1)) * live)
        lines.append(jnp.where(low1, pltpu.roll(re, 64, 1), im) * live)
    picked = []
    for m in range(4):
        out = jnp.zeros((1, 128), jnp.float32)
        for r in range(4):
            out = out + jnp.where(spin == (r ^ m), lines[r], 0.0)
        picked.append(out)
    for number in range(16):
        m, w = TABLE[number][0], TABLE[number][1]
        odd = jnp.zeros((1, 128), jnp.int32)
        for bit in range(2):
            if w >> bit & 1:
                odd = odd + (spin // (1 << bit)) % 2
        ltab[number] = jnp.where(odd == 1, -picked[m], picked[m])

    for g in range(NG):
        number = gid_ref[g]
        xbuf[2 * (g % 2), g // 2] = tabs[number, 0]
        xbuf[2 * (g % 2) + 1, g // 2] = tabs[number, 1]
        xl[g % 2, g // 2] = ltab[number]

    pl.semaphore_wait(barrier, len(partners))

    for j in range(NY):
        to_y = (y + ORDER[j]) % NY
        for k in range(1, NX):
            to_x = (x + k) % NX
            pltpu.make_async_remote_copy(
                src_ref=xbuf.at[to_x, to_y],
                dst_ref=xrecv.at[j, k - 1],
                send_sem=x_send,
                recv_sem=x_recv.at[j],
                device_id=at(y, to_x, zh, tm),
                device_id_type=MESH,
            ).start()
        if j == 0:
            for k in range(1, NX):
                to_x = (x + k) % NX
                pltpu.make_async_remote_copy(
                    src_ref=xl.at[to_x // 2],
                    dst_ref=xlrecv.at[k - 1],
                    send_sem=xl_send,
                    recv_sem=xl_recv,
                    device_id=at(y, to_x, zh, tm),
                    device_id_type=MESH,
                ).start()

    for j in range(NY):
        to_y = (y + ORDER[j]) % NY
        pltpu.make_async_copy(xrecv.at[j], xrecv.at[j], x_recv.at[j]).wait()
        ysend[j] = (xbuf[x, to_y] + xrecv[j, 0]) + (xrecv[j, 1] + xrecv[j, 2])
        pltpu.make_async_remote_copy(
            src_ref=ysend.at[j, pl.ds(8, 8)],
            dst_ref=yrecv2.at[j],
            send_sem=y2_send,
            recv_sem=y2_recv,
            device_id=at(to_y, xp, zh, tm),
            device_id_type=MESH,
        ).start()
        if j < NY - 1:
            pltpu.make_async_remote_copy(
                src_ref=ysend.at[j],
                dst_ref=yrecv.at[j],
                send_sem=y_send,
                recv_sem=y_recv,
                device_id=at(to_y, x, zh, tm),
                device_id_type=MESH,
            ).start()
        if j == 0:
            pltpu.make_async_copy(xlrecv, xlrecv, xl_recv).wait()
            yl[...] = (xl[x // 2] + xlrecv[0]) + (xlrecv[1] + xlrecv[2])
            for i in range(NY - 1):
                line_y = (y + ORDER[i]) % NY
                pltpu.make_async_remote_copy(
                    src_ref=yl.at[line_y],
                    dst_ref=ylrecv.at[i],
                    send_sem=yl_send,
                    recv_sem=yl_recv,
                    device_id=at(line_y, x, zh, tm),
                    device_id_type=MESH,
                ).start()

    pltpu.make_async_copy(ylrecv, ylrecv, yl_recv).wait()
    total = yl[y]
    for i in range(NY - 1):
        total = total + ylrecv[i]
    zl[...] = total
    zlrecv[zh * NTM + tm] = total
    for kz in range(NZH):
        for kt in range(NTM):
            if kz or kt:
                pltpu.make_async_remote_copy(
                    src_ref=zl,
                    dst_ref=zlrecv.at[zh * NTM + tm],
                    send_sem=zl_send,
                    recv_sem=zl_recv,
                    device_id=at(y, x, (zh + kz) % NZH, (tm + kt) % NTM),
                    device_id_type=MESH,
                ).start()

    pltpu.make_async_copy(yrecv, yrecv, y_recv).wait()
    pltpu.make_async_copy(yrecv2, yrecv2, y2_recv).wait()
    own = ysend[NY - 1]
    for j in range(NY - 1):
        own = own + yrecv[j]
    other = yrecv2[0]
    for j in range(1, NY):
        other = other + yrecv2[j]
    diag, off = own[0:8], own[8:16]
    first = p == 0
    left, right = jnp.where(first, diag, off), jnp.where(first, off, diag)
    upper, lower = jnp.where(first, diag, other), jnp.where(first, other, diag)

    def turned(tile, shift):
        shift = shift % 128
        return pltpu.roll(tile, shift, 1) if shift else tile

    columns = [turned(t, -32 * ib) for t in (upper, lower) for ib in range(4)]
    columns = jnp.concatenate(columns + columns, axis=0)
    flipped = columns.T
    for ib in range(4):
        r0 = 8 * ib
        rows = jnp.where(lane < 32, turned(left, -32 * ib), turned(right, 32 - 32 * ib))
        rows = jnp.where(low, rows, flipped[r0 : r0 + 8])
        zsend[ib // 2, 8 * (ib % 2) : 8 * (ib % 2) + 8, :] = rows
    zrecv[zh * NTM + tm] = zsend[zh]
    for kz in range(NZH):
        for kt in range(NTM):
            if kz or kt:
                to_z = (zh + kz) % NZH
                pltpu.make_async_remote_copy(
                    src_ref=zsend.at[to_z],
                    dst_ref=zrecv.at[zh * NTM + tm],
                    send_sem=z_send,
                    recv_sem=z_recv,
                    device_id=at(y, x, to_z, (tm + kt) % NTM),
                    device_id_type=MESH,
                ).start()

    number = gid_ref[2 * y + x // 2]
    half = 0.5 * gram_scale
    re_t = pick(number, [half * (t[2] - t[3]) for t in TABLE])
    re_f = pick(number, [half * t[4] * (t[2] + t[3]) for t in TABLE])
    im_t = pick(number, [half * (t[2] + t[3]) for t in TABLE])
    im_f = pick(number, [half * t[4] * (t[3] - t[2]) for t in TABLE])
    phase_re = pick(number, [float(t[2]) for t in TABLE])
    phase_im = pick(number, [float(t[3]) for t in TABLE])
    straight = jnp.where(low1, re_t, im_f)
    crossed = jnp.where(low1, re_f, im_t)
    turn = jnp.where(low1, -phase_im, phase_im)

    pltpu.make_async_copy(zlrecv.at[pl.ds(0, 15)], zlrecv.at[pl.ds(0, 15)], zl_recv).wait()
    value = (zlrecv[0:NTM] + zlrecv[NTM : 2 * NTM]).reshape(NTM, 128)
    value = phase_re * value + turn * pltpu.roll(value, 64, 1)
    value = pltpu.roll(value, (128 - 16 * (2 * p + zh)) % 128, 1)
    loop_ref[:, 0, :] = value[:, 0:16]
    loop_ref[:, 1, :] = value[:, 64:80]

    pltpu.make_async_copy(zrecv.at[pl.ds(0, 15)], zrecv.at[pl.ds(0, 15)], z_recv).wait()
    for t in range(NTM):
        value = zrecv[t] + zrecv[NTM + t]
        gram_ref[t] = straight * value + crossed * pltpu.roll(value, 64, 1)

    pltpu.make_async_copy(xbuf.at[pl.ds(0, 3)], xbuf.at[pl.ds(0, 3)], x_send).wait()
    pltpu.make_async_copy(xlrecv, xlrecv, xl_send).wait()
    pltpu.make_async_copy(yrecv, yrecv, y_send).wait()
    pltpu.make_async_copy(yrecv2, yrecv2, y2_send).wait()
    pltpu.make_async_copy(ylrecv, ylrecv, yl_send).wait()
    pltpu.make_async_copy(zrecv.at[pl.ds(0, 15)], zrecv.at[pl.ds(0, 15)], z_send).wait()
    pltpu.make_async_copy(zlrecv.at[pl.ds(0, 15)], zlrecv.at[pl.ds(0, 15)], zl_send).wait()


def shards(vectors, dilution, gamma_ids):
    slices, count, halves, comps, sites = vectors.shape
    total_sites = sites * lax.axis_size("space")
    gram_scale = 1.0 / math.sqrt(48.0 * total_sites)
    loop_scale = 1.0 / math.sqrt(1.0 * total_sites)
    flat = vectors.transpose(0, 1, 3, 2, 4).reshape(count * comps * halves, sites)
    f32, bf16 = jnp.float32, jnp.bfloat16
    dma = pltpu.SemaphoreType.DMA
    vmem = pltpu.VMEM
    gram, loops = pl.pallas_call(
        partial(kernel, gram_scale, loop_scale),
        out_shape=(
            jax.ShapeDtypeStruct((NTM, 16, 128), f32),
            jax.ShapeDtypeStruct((NTM, 2, 16), f32),
        ),
        in_specs=[
            pl.BlockSpec(memory_space=pltpu.SMEM),
            pl.BlockSpec(memory_space=pltpu.VMEM),
            pl.BlockSpec(memory_space=pl.ANY),
        ],
        out_specs=(
            pl.BlockSpec(memory_space=pltpu.VMEM),
            pl.BlockSpec(memory_space=pltpu.VMEM),
        ),
        scratch_shapes=[
            vmem((1536, 128), bf16),
            vmem((1536, 128), f32),
            vmem((528, 768), bf16),
            vmem((256, 256), f32),
            vmem((16, 2, 16, 128), f32),
            vmem((16, 1, 128), f32),
            vmem((NX, NY, 16, 128), f32),
            vmem((NY, NX - 1, 16, 128), f32),
            vmem((NY, 16, 128), f32),
            vmem((NY - 1, 16, 128), f32),
            vmem((NY, 8, 128), f32),
            vmem((NZH, 16, 128), f32),
            vmem((NZH * NTM, 16, 128), f32),
            vmem((2, NY, 1, 128), f32),
            vmem((NX - 1, NY, 1, 128), f32),
            vmem((NY, 1, 128), f32),
            vmem((NY - 1, 1, 128), f32),
            vmem((1, 128), f32),
            vmem((NZH * NTM, 1, 128), f32),
            dma,
            dma,
            dma((NY,)),
        ]
        + [dma] * 12,
        compiler_params=pltpu.CompilerParams(collective_id=0, has_side_effects=True),
        name="gram_loops",
    )(gamma_ids, dilution.reshape(1, count), flat)
    return gram, loops.transpose(0, 2, 1)


def solution(mesh):
    placed = (P("tm", None, None, None, "space"), P(), P())
    return jax.shard_map(
        shards,
        mesh=mesh,
        in_specs=placed,
        out_specs=(P(None, "space", None), P(None, "space", None)),
        check_vma=False,
    )
```

time: 87.2 us -> 34.3 us (0.39)
  Pallas kernels: 0 us -> 31.3 us
  blocking collectives: 30.9 us -> 0 us
  starting transfers between devices: 28 us -> 0 us
  waiting for transfers between devices: 11.8 us -> 0 us
  matrix products: 6.86 us -> 0 us
  local copies, waits for them, and re-layouts: 5.96 us -> 2.08 us
  other arithmetic: 2.42 us -> 0 us
    pallas_call x0 -> x1, Pallas kernels: none -> 31.3 us  [shards(): pl.pallas_call(partial(kernel, gram_scale, loop_scale), out_shape=(jax.Sh...]
    all_gather x2 -> x0, blocking collectives: 30.9 us -> none  [the longest x1 17.7 us: shards(): lax.all_gather(shares[0], 'tm', axis=0, tiled=True)]
    all_to_all x2 -> x0, starting transfers between devices: 28 us -> none  [sent_and_summed(): lax.all_to_all(tiles, axis, split_axis=0, concat_axis=0, tiled=True)]
    all_to_all x2 -> x0, waiting for transfers between devices: 11.8 us -> none  [sent_and_summed(): lax.all_to_all(tiles, axis, split_axis=0, concat_axis=0, tiled=True)]
    dot_general x13 -> x0, matrix products: 6.86 us -> none  [the longest x1 1.09 us: one_slice(): ein('gab,iajb->gij', gamma_imag, pair_real)]
    reduce_sum x3 -> x0, other arithmetic: 2.08 us -> none  [the longest x1 1.93 us: one_slice(): jnp.sum(block, axis=-1, dtype=jnp.float32).reshape(count, 2, 4, 3)]
    mul x2 -> x0, local copies, waits for them, and re-layouts: 1.69 us -> none  [the longest x1 0.95 us: one_slice(): gram = gram * gram_scale]
    unnamed x15 -> x4, local copies, waits for them, and re-layouts: 3.11 us -> 2.08 us
  transfers between devices with their start and end apart: 2 -> 0, of which waited for: 2 -> 0; matrix products, arithmetic and copies ran while one was open for 9% -> 0% of each run, Pallas kernels for 0% -> 0%
where the time goes in v1:
time: 34.3 us; the launch traced here: 34 us
  Pallas kernels  31.3 us (91%)
  local copies, waits for them, and re-layouts  2.08 us (6%)
  between operations  0.65 us (2%)
    pallas_call x1, Pallas kernels, shards(): pl.pallas_call(partial(kernel, gram_scale, loop_scale), out_shape=(jax.Sh...  31.3 us
    unnamed x4, local copies, waits for them, and re-layouts  2.08 us

profile of v1, /device:TPU:1, one launch (start us, length us, event | category | flops | bytes accessed | tf_op | source)
XLA Modules:
  0.0 34.0 jit_solution(5958874886602375697)
XLA Ops:
  0.6 31.3 %gram_loops.1 = (f32[8,16,128]{2,1,0:T(8,128)}, f32[8,2,16]{2,1,0:T(2,128)}) custom-call(s32[16]{0:T(128)} %gid_ref.1, s32[1,64]{1,0:T(1,128)} %bitcast.7, bf16[1536,128]{1,0:T(8,128)(2,1)} %bitcast.5), custom_call_target="tpu_custom_call" | custom-call | tf_op jit(solution)/shard_map/gram_loops/pallas_call | solution.py:389
  32.0 0.0 copy-start
  32.0 1.5 %copy.7 = f32[8,16,128]{2,1,0:T(8,128)} copy(f32[8,16,128]{2,1,0:T(8,128)} %get-tuple-element.8) | data formatting | bytes 131072
  33.4 0.0 copy-done
  33.4 0.6 %copy.8 = f32[8,16,2]{1,2,0:T(2,128)} copy(f32[8,16,2]{1,2,0:T(2,128)S(1)} %bitcast.6) | data formatting | bytes 2048
Async XLA Ops:
  32.0 1.5 %copy-start = (f32[8,2,16]{2,1,0:T(2,128)S(1)}, f32[8,2,16]{2,1,0:T(2,128)}, u32[]{:S(2)}) copy-start(f32[8,2,16]{2,1,0:T(2,128)} %get-tuple-element.5) | copy-start | bytes 3076

commit v2 on v1

--- a/solution.py
+++ b/solution.py
@@ -62,11 +62,13 @@
 def kernel(
     gram_scale,
     loop_scale,
-    gid_ref,
-    dil_ref,
+    gid_hbm,
+    dil_hbm,
     v_hbm,
     gram_ref,
     loop_ref,
+    gid_ref,
+    dil_ref,
     vb,
     vf,
     lhs,
@@ -87,6 +89,8 @@
     zl,
     zlrecv,
     in_sem,
+    gid_sem,
+    dil_sem,
     x_send,
     x_recv,
     y_send,
@@ -112,6 +116,10 @@
 
     load = pltpu.make_async_copy(v_hbm, vb, in_sem)
     load.start()
+    load_gid = pltpu.make_async_copy(gid_hbm, gid_ref, gid_sem)
+    load_gid.start()
+    load_dil = pltpu.make_async_copy(dil_hbm, dil_ref, dil_sem)
+    load_dil.start()
 
     def at(y_, x_, zh_, tm_):
         return (y_ * 8 + x_ * 2 + zh_, tm_)
@@ -184,6 +192,7 @@
                     if TABLE[number][0] == m:
                         tabs[number, pp, 8 * slot : 8 * slot + 8, :] = combos[TABLE[number][1]]
 
+    load_dil.wait()
     dil = dil_ref[...]
     dil = jnp.concatenate([dil, dil], axis=1)
     klass = (dil >= 12).astype(jnp.int32)
@@ -220,6 +229,7 @@
                 odd = odd + (spin // (1 << bit)) % 2
         ltab[number] = jnp.where(odd == 1, -picked[m], picked[m])
 
+    load_gid.wait()
     for g in range(NG):
         number = gid_ref[g]
         xbuf[2 * (g % 2), g // 2] = tabs[number, 0]
@@ -383,6 +393,7 @@
     gram_scale = 1.0 / math.sqrt(48.0 * total_sites)
     loop_scale = 1.0 / math.sqrt(1.0 * total_sites)
     flat = vectors.transpose(0, 1, 3, 2, 4).reshape(count * comps * halves, sites)
+    operands = (gamma_ids, dilution.reshape(1, count), flat)
     f32, bf16 = jnp.float32, jnp.bfloat16
     dma = pltpu.SemaphoreType.DMA
     vmem = pltpu.VMEM
@@ -393,15 +404,17 @@
             jax.ShapeDtypeStruct((NTM, 2, 16), f32),
         ),
         in_specs=[
-            pl.BlockSpec(memory_space=pltpu.SMEM),
-            pl.BlockSpec(memory_space=pltpu.VMEM),
-            pl.BlockSpec(memory_space=pl.ANY),
+            pl.BlockSpec(memory_space=pltpu.HBM),
+            pl.BlockSpec(memory_space=pltpu.HBM),
+            pl.BlockSpec(memory_space=pltpu.HBM),
         ],
         out_specs=(
             pl.BlockSpec(memory_space=pltpu.VMEM),
             pl.BlockSpec(memory_space=pltpu.VMEM),
         ),
         scratch_shapes=[
+            pltpu.SMEM((NG,), jnp.int32),
+            vmem((1, NV), jnp.int32),
             vmem((1536, 128), bf16),
             vmem((1536, 128), f32),
             vmem((528, 768), bf16),
@@ -423,12 +436,16 @@
             vmem((NZH * NTM, 1, 128), f32),
             dma,
             dma,
+            dma,
+            dma,
             dma((NY,)),
         ]
         + [dma] * 12,
-        compiler_params=pltpu.CompilerParams(collective_id=0, has_side_effects=True),
+        compiler_params=pltpu.CompilerParams(
+            collective_id=0, has_side_effects=True, vmem_limit_bytes=8 << 20
+        ),
         name="gram_loops",
-    )(gamma_ids, dilution.reshape(1, count), flat)
+    )(*[pltpu.with_memory_space_constraint(a, pltpu.HBM) for a in operands])
     return gram, loops.transpose(0, 2, 1)
 
 

time: 34.3 us -> 32.1 us (0.936)
  Pallas kernels: 31.3 us -> 30.1 us
  local copies, waits for them, and re-layouts: 2.08 us -> 1.23 us
    pallas_call x1, Pallas kernels: 31.3 us -> 30.1 us  [shards(): pl.pallas_call(partial(kernel, gram_scale, loop_scale), out_shape=(jax.Sh...]
    unnamed x4 -> x2, local copies, waits for them, and re-layouts: 2.08 us -> 1.23 us
where the time goes in v2:
time: 32.1 us; the launch traced here: 31.9 us
  Pallas kernels  30.1 us (94%)
  local copies, waits for them, and re-layouts  1.23 us (4%)
  between operations  0.64 us (2%)
    pallas_call x1, Pallas kernels, shards(): pl.pallas_call(partial(kernel, gram_scale, loop_scale), out_shape=(jax.Sh...  30.1 us
    unnamed x2, local copies, waits for them, and re-layouts  1.23 us

profile of v2, /device:TPU:1, one launch (start us, length us, event | category | flops | bytes accessed | tf_op | source)
XLA Modules:
  0.0 31.9 jit_solution(2629551718890712246)
XLA Ops:
  0.6 30.1 %gram_loops.1 = (f32[8,16,128]{2,1,0:T(8,128)S(1)}, f32[8,2,16]{2,1,0:T(2,128)S(1)}) custom-call(s32[16]{0:T(128)} %gid_hbm.1, s32[1,64]{1,0:T(1,128)} %bitcast.7, bf16[1536,128]{1,0:T(8,128)(2,1)} %bitcast.6), custom_call_target="tpu_custom_call" | custom-call | tf_op jit(solution)/shard_map/gram_loops/pallas_call | solution.py:400
  30.7 0.6 %copy.7 = f32[8,16,128]{2,1,0:T(8,128)} copy(f32[8,16,128]{2,1,0:T(8,128)S(1)} %get-tuple-element.8) | data formatting | bytes 131072
  31.3 0.6 %copy.8 = f32[8,16,2]{1,2,0:T(2,128)} copy(f32[8,16,2]{1,2,0:T(2,128)S(1)} %bitcast.5) | data formatting | bytes 2048
